TPU v7x, 256 devices: a whole 4x4x8 slice. The times are simulated.
256 devices in a mesh: row: 8 (over y_lo, x), col: 32 (over y_hi, z, core).
Axes of the slice: x: 4, y: 4 (y_hi: 2, y_lo: 2; y = y_hi * 2 + y_lo), z: 8, core: 2. Of those that a mesh axis runs over, the one named last changes fastest.
Arguments:
- density: float32 [256, 256, 256], P('col', 'row'), may hold values from 0.5 to 2
- velocity: float32 [3, 256, 256, 256], P(None, 'col', 'row'), may hold values from -0.6 to 0.6
- pressure: float32 [256, 256, 256], P('col', 'row'), may hold values from 1 to 2
- face_field: float32 [3, 256, 256, 256], P(None, 'col', 'row'), may hold values from -0.6 to 0.6
Outputs:
- new_density: float32 [256, 256, 256], P('col', 'row')
- new_momentum: float32 [3, 256, 256, 256], P(None, 'col', 'row')
- new_energy: float32 [256, 256, 256], P('col', 'row')
- new_face_field: float32 [3, 256, 256, 256], P(None, 'col', 'row')
All inputs are finite; a program needn't handle non-finite values.
Results may differ from a plain program's by a relative error of at most 0.0003.
Values sent between devices are 32-bit elements; how exact they have to be, the bound alone decides.
A program may use at most 64 MiB of HBM per device.

v0:
```python
import functools
import math

import jax
import jax.numpy as jnp
import numpy as np
from jax import lax
from jax.experimental import pallas as pl
from jax.experimental.pallas import tpu as pltpu
from jax.sharding import PartitionSpec as P

gamma_gas = 5.0 / 3.0
time_step = 0.1
coupling = 3.0


def tables(size, chunk):
    index = np.arange(size)
    angle = (index[:, None] * index[None, :] % size) * (2.0 * math.pi / size)
    natural = np.cos(angle) + np.sin(angle)
    order = np.arange(size).reshape(size // chunk, chunk).T.reshape(-1)
    values = 2.0 * np.cos(index * (2.0 * math.pi / size)) - 2.0
    as32 = lambda x: np.ascontiguousarray(x, dtype=np.float32)
    return (as32(natural), as32(natural[:, order]), as32(natural[order, :]), values)


def mm(a, b):
    return lax.dot_general(
        a,
        b,
        (((1,), (0,)), ((), ())),
        precision=lax.Precision.HIGHEST,
        preferred_element_type=jnp.float32,
    )


def exchange_chunks(parts):
    flat = []
    for i in range(4):
        flat.append((parts[i][0], parts[i + 4][0]))
    for i in range(4):
        flat.append((parts[i][1], parts[i + 4][1]))
    rows = parts[0][0].shape[0]
    lane = lax.broadcasted_iota(jnp.int32, (rows, 128), 1)
    for bit, width in ((2, 64), (1, 32)):
        keep = (lane // width) % 2 == 0
        fresh = [None] * 8
        for i in range(8):
            if i & bit:
                continue
            j = i | bit
            low, high = flat[i], flat[j]
            fresh[i] = tuple(
                jnp.where(keep, low[h], pltpu.roll(high[h], width, 1)) for h in range(2)
            )
            fresh[j] = tuple(
                jnp.where(keep, pltpu.roll(low[h], 128 - width, 1), high[h]) for h in range(2)
            )
        flat = fresh
    return flat


def shift_x_down(x):
    return pltpu.roll(x, 1, 1)


def shift_x_up(x):
    return pltpu.roll(x, 255, 1)


def side_terms(side, normal, normal_sq):
    dens, vel_n, vel_a, vel_b, pres, field_a, field_b, inv_dens, sound, hydro = side
    across = field_a * field_a + field_b * field_b
    magnetic = 0.5 * (normal_sq + across)
    energy = hydro + magnetic
    total_p = pres + magnetic
    dot_vb = vel_n * normal + vel_a * field_a + vel_b * field_b
    along = normal_sq * inv_dens
    across = across * inv_dens
    gap = sound - along - across
    fast_sq = sound + along + across + jnp.sqrt(gap * gap + 4.0 * sound * across)
    return (energy, total_p, dot_vb, fast_sq)


def star_state(side, normal, normal_sq, energy, total_p, dot_vb, relative, mass, edge, middle, star_p):
    dens, vel_n, vel_a, vel_b, pres, field_a, field_b = side[:7]
    edge_gap = edge - middle
    inv_gap = 1.0 / edge_gap
    inv_div = 1.0 / (mass * edge_gap - normal_sq)
    star_dens = mass * inv_gap
    offset = normal * (middle - vel_n) * inv_div
    star_va = vel_a - field_a * offset
    star_vb = vel_b - field_b * offset
    factor = (mass * relative - normal_sq) * inv_div
    star_fa = field_a * factor
    star_fb = field_b * factor
    star_dot = middle * normal + star_va * star_fa + star_vb * star_fb
    star_energy = (
        relative * energy - total_p * vel_n + star_p * middle + normal * (dot_vb - star_dot)
    ) * inv_gap
    return (star_dens, star_va, star_vb, star_fa, star_fb, star_dot, star_energy, jnp.sqrt(star_dens))


def hlld_flux(left, right, normal):
    normal_sq = normal * normal
    energy_l, total_l, dot_l, fast_l = side_terms(left, normal, normal_sq)
    energy_r, total_r, dot_r, fast_r = side_terms(right, normal, normal_sq)
    fastest = jnp.sqrt(0.5 * jnp.maximum(fast_l, fast_r))
    slow_edge = jnp.minimum(left[1], right[1]) - fastest
    fast_edge = jnp.maximum(left[1], right[1]) + fastest
    rel_l = slow_edge - left[1]
    rel_r = fast_edge - right[1]
    mass_l = left[0] * rel_l
    mass_r = right[0] * rel_r
    inv_weight = 1.0 / (mass_r - mass_l)
    middle = (mass_r * right[1] - mass_l * left[1] - total_r + total_l) * inv_weight
    star_p = (
        mass_r * total_l - mass_l * total_r + mass_l * mass_r * (right[1] - left[1])
    ) * inv_weight
    star_l = star_state(
        left, normal, normal_sq, energy_l, total_l, dot_l, rel_l, mass_l, slow_edge, middle, star_p
    )
    star_r = star_state(
        right, normal, normal_sq, energy_r, total_r, dot_r, rel_r, mass_r, fast_edge, middle, star_p
    )
    root_l, root_r = star_l[7], star_r[7]
    orient = jnp.where(normal > 0.0, 1.0, jnp.where(normal < 0.0, -1.0, 0.0))
    inv_sum = 1.0 / (root_l + root_r)
    both = root_l * root_r * orient
    dbl_va = (root_l * star_l[1] + root_r * star_r[1] + (star_r[3] - star_l[3]) * orient) * inv_sum
    dbl_vb = (root_l * star_l[2] + root_r * star_r[2] + (star_r[4] - star_l[4]) * orient) * inv_sum
    dbl_fa = (root_l * star_r[3] + root_r * star_l[3] + both * (star_r[1] - star_l[1])) * inv_sum
    dbl_fb = (root_l * star_r[4] + root_r * star_l[4] + both * (star_r[2] - star_l[2])) * inv_sum
    dbl_dot = middle * normal + dbl_va * dbl_fa + dbl_vb * dbl_fb
    on_left = (middle > 0.0) | (slow_edge > 0.0)

    def pick(low, high):
        return jnp.where(on_left, low, high)

    dens, vel_n, vel_a, vel_b = [pick(left[i], right[i]) for i in range(4)]
    field_a, field_b = [pick(left[i], right[i]) for i in (5, 6)]
    energy = pick(energy_l, energy_r)
    total_p = pick(total_l, total_r)
    dot_vb = pick(dot_l, dot_r)
    edge = pick(slow_edge, fast_edge)
    s_dens, s_va, s_vb, s_fa, s_fb, s_dot, s_energy, root = [
        pick(low, high) for low, high in zip(star_l, star_r)
    ]
    way = pick(-1.0, 1.0)
    inner = middle + way * jnp.abs(normal) / root
    ahead = inner > 0.0
    outer = (on_left & (slow_edge > 0.0)) | ~(on_left | (fast_edge > 0.0) | ahead)
    double = (on_left ^ ahead) & ~outer
    d_energy = s_energy + way * root * (s_dot - dbl_dot) * orient
    to_star = jnp.where(outer, 0.0, edge)
    to_double = jnp.where(double, inner, 0.0)
    mass = dens * vel_n
    return (
        mass + to_star * (s_dens - dens),
        mass * vel_n + total_p - normal_sq + to_star * (s_dens * middle - mass),
        mass * vel_a
        - normal * field_a
        + to_star * (s_dens * s_va - dens * vel_a)
        + to_double * (s_dens * (dbl_va - s_va)),
        mass * vel_b
        - normal * field_b
        + to_star * (s_dens * s_vb - dens * vel_b)
        + to_double * (s_dens * (dbl_vb - s_vb)),
        (energy + total_p) * vel_n
        - normal * dot_vb
        + to_star * (s_energy - energy)
        + to_double * (d_energy - s_energy),
        field_a * vel_n - normal * vel_a + to_star * (s_fa - field_a) + to_double * (dbl_fa - s_fa),
        field_b * vel_n - normal * vel_b + to_star * (s_fb - field_b) + to_double * (dbl_fb - s_fb),
    )


def sublane_is(which):
    return lax.broadcasted_iota(jnp.int32, (8, 256), 0) == which


def row_before(load, base, tile):
    mixed = jnp.where(sublane_is(7), load(base + lax.rem(tile + 4, 5)), load(base + tile))
    return pltpu.roll(mixed, 1, 0)


def row_after(load, base, tile):
    mixed = jnp.where(sublane_is(0), load(base + lax.rem(tile + 1, 5)), load(base + tile))
    return pltpu.roll(mixed, 7, 0)


tangents = ((1, 2), (2, 0), (0, 1))


def cell_pass(state, above, cell, base, tile):
    at = base + tile
    dens = state[0, at]
    vel = [state[1 + c, at] for c in range(3)]
    pres = state[4, at]
    cell[0, at] = 0.5 * (state[5, at] + shift_x_up(state[5, at]))
    cell[1, at] = 0.5 * (state[6, at] + row_after(lambda i: state[6, i], base, tile))
    cell[2, at] = 0.5 * (state[7, at] + above)
    inv_dens = 1.0 / dens
    cell[3, at] = inv_dens
    cell[4, at] = gamma_gas * pres * inv_dens
    cell[5, at] = pres / (gamma_gas - 1.0) + 0.5 * dens * (
        vel[0] * vel[0] + vel[1] * vel[1] + vel[2] * vel[2]
    )


def flux_pass(direction, state, cell, flux, base, tile):
    at = base + tile
    first, second = tangents[direction]
    members = (
        (state, 0),
        (state, 1 + direction),
        (state, 1 + first),
        (state, 1 + second),
        (state, 4),
        (cell, first),
        (cell, second),
        (cell, 3),
        (cell, 4),
        (cell, 5),
    )
    right = [ref[f, at] for ref, f in members]
    if direction == 0:
        left = [shift_x_down(value) for value in right]
    elif direction == 1:
        left = [row_before(lambda i, ref=ref, f=f: ref[f, i], base, tile) for ref, f in members]
    else:
        left = [ref[f, at - 5] for ref, f in members]
    result = hlld_flux(left, right, state[5 + direction, at])
    for member in range(7):
        flux[direction, member, at] = result[member]


def edge_pass(flux, edge, base, tile):
    at = base + tile
    edge[2, at] = 0.25 * (
        flux[1, 6, at]
        + shift_x_down(flux[1, 6, at])
        - flux[0, 5, at]
        - row_before(lambda i: flux[0, 5, i], base, tile)
    )
    edge[0, at] = 0.25 * (
        flux[2, 6, at]
        + row_before(lambda i: flux[2, 6, i], base, tile)
        - flux[1, 5, at]
        - flux[1, 5, at - 5]
    )
    edge[1, at] = 0.25 * (
        flux[0, 6, at] + flux[0, 6, at - 5] - flux[2, 5, at] - shift_x_down(flux[2, 5, at])
    )


def update_pass(state, cell, flux, edge, outs, base, tile, plane):
    new_dens, new_mom, new_energy, new_face = outs
    at = base + tile

    def change(slots):
        low = flux[0, slots[0], at]
        total = shift_x_up(low) - low
        total += row_after(lambda i: flux[1, slots[1], i], base, tile) - flux[1, slots[1], at]
        return total + (flux[2, slots[2], at + 5] - flux[2, slots[2], at])

    dens = state[0, at]
    new_dens[plane, tile] = dens - time_step * change((0, 0, 0))
    slots = ((1, 3, 2), (2, 1, 3), (3, 2, 1))
    for c in range(3):
        new_mom[c, plane, tile] = dens * state[1 + c, at] - time_step * change(slots[c])
    field = [cell[c, at] for c in range(3)]
    energy = cell[5, at] + 0.5 * (field[0] * field[0] + field[1] * field[1] + field[2] * field[2])
    new_energy[plane, tile] = energy - time_step * change((4, 4, 4))
    low = [edge[c, at] for c in range(3)]
    new_face[0, plane, tile] = state[5, at] - time_step * (
        row_after(lambda i: edge[2, i], base, tile) - low[2] - (edge[1, at + 5] - low[1])
    )
    new_face[1, plane, tile] = state[6, at] - time_step * (
        edge[0, at + 5] - low[0] - (shift_x_up(low[2]) - low[2])
    )
    new_face[2, plane, tile] = state[7, at] - time_step * (
        shift_x_up(low[1]) - low[1] - (row_after(lambda i: edge[0, i], base, tile) - low[0])
    )


def pull_pass(state, phi, outs, base, tile, plane):
    new_dens, new_mom, new_energy, new_face = outs
    at = base + tile
    centre = phi[at]
    load = lambda i: phi[i]
    accel = (
        -0.5 * (shift_x_up(centre) - shift_x_down(centre)),
        -0.5 * (row_after(load, base, tile) - row_before(load, base, tile)),
        -0.5 * (phi[at + 5] - phi[at - 5]),
    )
    pulled = time_step * state[0, at]
    work = jnp.zeros_like(centre)
    for c in range(3):
        new_mom[c, plane, tile] += pulled * accel[c]
        work += pulled * state[1 + c, at] * accel[c]
    new_energy[plane, tile] += work


def step_kernel(
    rows, cols, dens, vel, pres, face, nat, perm_c, perm_r, eig_z, eig_y, eig_x,
    new_dens, new_mom, new_energy, new_face,
    send_a, recv_a, send_c, recv_c, send_e, recv_e, send_g, recv_g,
    state, cell, flux, edge, phi, above_bz, rim_out, rim_in, phi_out, phi_in,
    sa, ra, sc, rc, se, re, sg, rg, halo_s, halo_r,
):
    row = lax.axis_index("row")
    col = lax.axis_index("col")
    outs = (new_dens, new_mom, new_energy, new_face)
    barrier = pltpu.get_barrier_semaphore()
    row_up = lax.rem(row + 1, rows)
    row_down = lax.rem(row + rows - 1, rows)
    col_up = lax.rem(col + 1, cols)
    col_down = lax.rem(col + cols - 1, cols)

    def copy(src, dst, send, recv, to_row, to_col):
        return pltpu.make_async_remote_copy(
            src_ref=src, dst_ref=dst, send_sem=send, recv_sem=recv,
            device_id={"row": to_row, "col": to_col}, device_id_type=pl.DeviceIdType.MESH,
        )

    def signal(to_row, to_col):
        pl.semaphore_signal(
            barrier, inc=1, device_id={"row": to_row, "col": to_col},
            device_id_type=pl.DeviceIdType.MESH,
        )

    @pl.loop(1, rows)
    def _(s):
        signal(lax.rem(row + s, rows), col)

    @pl.loop(1, cols)
    def _(s):
        signal(row, lax.rem(col + s, cols))

    def row_copy(peer, src, dst, ss, rs, slot):
        return copy(src.at[peer], dst.at[slot], ss.at[peer], rs.at[slot], peer, col)

    def col_copy(peer, src, dst, ss, rs, slot):
        return copy(src.at[:, peer], dst.at[:, slot], ss.at[peer], rs.at[slot], row, peer)

    def start_row(*refs):
        @pl.loop(1, rows)
        def _(s):
            row_copy(lax.rem(row + s, rows), *refs, row).start()

    def start_col(*refs):
        @pl.loop(1, cols)
        def _(s):
            col_copy(lax.rem(col + s, cols), *refs, col).start()

    def wait_row(*refs):
        @pl.loop(1, rows)
        def _(s):
            peer = lax.rem(row + s, rows)
            row_copy(peer, *refs, peer).wait_recv()

    def wait_col(*refs):
        @pl.loop(1, cols)
        def _(s):
            peer = lax.rem(col + s, cols)
            col_copy(peer, *refs, peer).wait_recv()

    over_a = (send_a, recv_a, sa, ra)
    over_c = (send_c, recv_c, sc, rc)
    over_e = (send_e, recv_e, se, re)
    over_g = (send_g, recv_g, sg, rg)

    def halo(number, src, dst, to_row, to_col):
        return copy(src, dst, halo_s.at[number], halo_r.at[number], to_row, to_col)

    rims = (
        halo(0, rim_out.at[0], rim_in.at[0], row_down, col),
        halo(1, rim_out.at[1], rim_in.at[1], row_up, col),
    )
    layers = []
    for number, (layer, base, to_col) in enumerate(((7, 0, col_up), (0, 45, col_down))):
        at = 2 + 5 * number
        layers += [
            halo(at, dens.at[layer], state.at[0, base : base + 4], row, to_col),
            halo(at + 1, vel.at[:, layer], state.at[1:4, base : base + 4], row, to_col),
            halo(at + 2, pres.at[layer], state.at[4, base : base + 4], row, to_col),
            halo(at + 3, face.at[:, layer], state.at[5:8, base : base + 4], row, to_col),
        ]
    layers.append(halo(6, face.at[2, 1], above_bz.at[0:4], row, col_down))
    corners = (
        halo(11, state.at[:, 44], state.at[:, 4], row, col_up),
        halo(12, state.at[:, 9], state.at[:, 49], row, col_down),
        halo(13, state.at[7, 14], above_bz.at[4], row, col_down),
    )
    phi_rims = (
        halo(14, phi_out.at[0], phi_in.at[0], row_down, col),
        halo(15, phi_out.at[1], phi_in.at[1], row_up, col),
    )
    phi_layers = (
        halo(16, phi.at[40:44], phi.at[0:4], row, col_up),
        halo(17, phi.at[5:9], phi.at[45:49], row, col_down),
    )

    spec = mm(dens[...].reshape(256, 256), nat[...])
    parts = [(spec[32 * z : 32 * z + 32, :128], spec[32 * z : 32 * z + 32, 128:]) for z in range(8)]
    parts = exchange_chunks(parts)
    for r in range(8):
        for h in range(2):
            send_a[r, :, 128 * h : 128 * h + 128] = parts[r][h]
    recv_a[row] = send_a[row]
    for f in range(8):
        source = dens if f == 0 else vel.at[f - 1] if f < 4 else pres if f == 4 else face.at[f - 5]
        rim_out[0, f] = source[:, 0, 0, :]
        rim_out[1, f] = source[:, 3, 7, :]
        for k in range(8):
            state[f, 5 * k + 5 : 5 * k + 9] = source[k]
    rim_out[0, 8] = face[1, :, 0, 1, :]
    rim_out[1, 8] = face[1, :, 0, 1, :]
    pl.semaphore_wait(barrier, rows + cols - 2)

    start_row(*over_a)
    for one in rims:
        one.start()
    for one in layers:
        one.start()
    for one in rims:
        one.wait_recv()
    sub = lax.broadcasted_iota(jnp.int32, (8, 256), 0)
    for f in range(8):
        second = rim_in[0, 8] if f == 6 else rim_in[0, f]
        first = rim_in[0, f]
        last = rim_in[1, f]
        for k in range(8):
            tile = jnp.where(sub == 0, first[k : k + 1], last[k : k + 1])
            if f == 6:
                tile = jnp.where(sub == 1, second[k : k + 1], tile)
            state[f, 5 * k + 9] = tile
    for one in corners:
        one.start()
    wait_row(*over_a)

    spec = mm(nat[...], recv_a[...].reshape(256, 256))
    for h in range(2):
        send_c[h] = spec[:, 128 * h : 128 * h + 128].reshape(32, 8, 128)
    recv_c[:, col] = send_c[:, col]
    start_col(*over_c)
    for one in layers:
        one.wait_recv()
    for one in corners:
        one.wait_recv()

    @pl.loop(0, 9)
    def _(plane):
        @pl.loop(0, 5)
        def _(tile):
            cell_pass(state, state[7, plane * 5 + tile + 5], cell, plane * 5, tile)

    @pl.loop(0, 5)
    def _(tile):
        cell_pass(state, above_bz[tile], cell, 45, tile)

    def fluxes(direction, low, high):
        @pl.loop(low, high)
        def _(plane):
            @pl.loop(0, 5)
            def _(tile):
                flux_pass(direction, state, cell, flux, plane * 5, tile)

    fluxes(0, 0, 10)
    fluxes(1, 0, 4)
    wait_col(*over_c)

    parts = [tuple(recv_c.at[h][:, y, :] for h in range(2)) for y in range(8)]
    parts = exchange_chunks(parts)
    full = jnp.concatenate([jnp.concatenate(list(p), axis=1) for p in parts], axis=0)
    full = mm(perm_c[...], full)
    total = eig_z[...] + (eig_y[pl.ds(col, 1), :] + eig_x[pl.ds(row, 1), :])
    kz = lax.broadcasted_iota(jnp.int32, (256, 256), 0)
    lane = lax.broadcasted_iota(jnp.int32, (256, 256), 1)
    anchor = kz + lane + row + col == 0
    full = full * jnp.where(anchor, 0.0, (coupling / 2.0**24) / jnp.where(anchor, 1.0, total))
    full = mm(perm_r[...], full)
    parts = [(full[32 * z : 32 * z + 32, :128], full[32 * z : 32 * z + 32, 128:]) for z in range(8)]
    parts = exchange_chunks(parts)
    for y in range(8):
        for h in range(2):
            send_e[h, :, y, :] = parts[y][h]
    recv_e[:, col] = send_e[:, col]
    start_col(*over_e)
    fluxes(1, 4, 10)
    fluxes(2, 1, 10)
    wait_col(*over_e)
    full = jnp.concatenate([recv_e[h].reshape(256, 128) for h in range(2)], axis=1)
    full = mm(nat[...], full)
    send_g[...] = full.reshape(8, 32, 256)
    recv_g[row] = send_g[row]
    start_row(*over_g)

    @pl.loop(1, 10)
    def _(plane):
        @pl.loop(0, 5)
        def _(tile):
            edge_pass(flux, edge, plane * 5, tile)

    @pl.loop(0, 8)
    def _(plane):
        @pl.loop(0, 4)
        def _(tile):
            update_pass(state, cell, flux, edge, outs, plane * 5 + 5, tile, plane)

    wait_row(*over_g)
    parts = [(recv_g[r, :, :128], recv_g[r, :, 128:]) for r in range(8)]
    parts = exchange_chunks(parts)
    full = jnp.concatenate([jnp.concatenate(list(p), axis=1) for p in parts], axis=0)
    full = mm(full, nat[...]).reshape(8, 4, 8, 256)
    for k in range(8):
        phi[5 * k + 5 : 5 * k + 9] = full[k]
    phi_out[0] = full[:, 0, 0, :]
    phi_out[1] = full[:, 3, 7, :]
    for one in phi_rims:
        one.start()
    for one in phi_layers:
        one.start()
    for one in phi_rims:
        one.wait_recv()
    for k in range(8):
        phi[5 * k + 9] = jnp.where(sub == 0, phi_in[0, k : k + 1], phi_in[1, k : k + 1])
    for one in phi_layers:
        one.wait_recv()

    @pl.loop(0, 8)
    def _(plane):
        @pl.loop(0, 4)
        def _(tile):
            pull_pass(state, phi, outs, plane * 5 + 5, tile, plane)

    @pl.loop(1, rows)
    def _(s):
        peer = lax.rem(row + s, rows)
        row_copy(peer, *over_a, row).wait_send()
        row_copy(peer, *over_g, row).wait_send()

    @pl.loop(1, cols)
    def _(s):
        peer = lax.rem(col + s, cols)
        col_copy(peer, *over_c, col).wait_send()
        col_copy(peer, *over_e, col).wait_send()

    for one in (*rims, *layers, *corners, *phi_rims, *phi_layers):
        one.wait_send()


def local(density, velocity, pressure, face_field):
    rows = lax.axis_size("row")
    cols = lax.axis_size("col")
    nat, perm_c, perm_r, values = tables(256, 8)
    eig_z = np.ascontiguousarray(np.broadcast_to(values[:, None], (256, 256)), dtype=np.float32)
    eig_y = np.repeat(values.reshape(32, 8), 32, axis=1).astype(np.float32)
    eig_x = np.tile(values.reshape(8, 32), (1, 8)).astype(np.float32)
    dma = pltpu.SemaphoreType.DMA
    vm = pltpu.VMEM
    f = jnp.float32
    block = (8, 4, 8, 256)
    scalar = jax.ShapeDtypeStruct(block, f)
    vector = jax.ShapeDtypeStruct((3, *block), f)
    results = pl.pallas_call(
        functools.partial(step_kernel, rows, cols),
        out_shape=(scalar, vector, scalar, vector),
        in_specs=[pl.BlockSpec(memory_space=vm)] * 10,
        out_specs=(pl.BlockSpec(memory_space=vm),) * 4,
        scratch_shapes=[
            vm((8, 32, 256), f), vm((8, 32, 256), f),
            vm((2, 32, 8, 128), f), vm((2, 32, 8, 128), f),
            vm((2, 32, 8, 128), f), vm((2, 32, 8, 128), f),
            vm((8, 32, 256), f), vm((8, 32, 256), f),
            vm((8, 50, 8, 256), f), vm((6, 50, 8, 256), f),
            vm((3, 7, 50, 8, 256), f), vm((3, 50, 8, 256), f),
            vm((50, 8, 256), f), vm((5, 8, 256), f),
            vm((2, 9, 8, 256), f), vm((2, 9, 8, 256), f),
            vm((2, 8, 256), f), vm((2, 8, 256), f),
            dma((8,)), dma((8,)), dma((32,)), dma((32,)),
            dma((32,)), dma((32,)), dma((8,)), dma((8,)),
            dma((18,)), dma((18,)),
        ],
        compiler_params=pltpu.CompilerParams(collective_id=0, has_side_effects=True, vmem_limit_bytes=60 * 1024 * 1024),
        name="step",
    )(
        density.reshape(block), velocity.reshape(3, *block), pressure.reshape(block),
        face_field.reshape(3, *block), jnp.asarray(nat), jnp.asarray(perm_c), jnp.asarray(perm_r),
        jnp.asarray(eig_z), jnp.asarray(eig_y), jnp.asarray(eig_x),
    )
    return (
        results[0].reshape(density.shape),
        results[1].reshape(velocity.shape),
        results[2].reshape(density.shape),
        results[3].reshape(velocity.shape),
    )


def solution(mesh):
    in_specs = (
        P("col", "row", None),
        P(None, "col", "row", None),
        P("col", "row", None),
        P(None, "col", "row", None),
    )
    out_specs = (
        P("col", "row", None),
        P(None, "col", "row", None),
        P("col", "row", None),
        P(None, "col", "row", None),
    )
    return jax.shard_map(local, mesh=mesh, in_specs=in_specs, out_specs=out_specs, check_vma=False)
```

profile of v0, /device:TPU:6, one launch (start us, length us, event | category | flops | bytes accessed | tf_op | source)
XLA Modules:
  0.0 76.5 jit_solution(11801370529680998093)
XLA Ops:
  0.6 70.4 %step.1 = (f32[8,4,8,256]{3,2,1,0:T(8,128)}, f32[3,8,4,8,256]{4,3,2,1,0:T(8,128)}, f32[8,4,8,256]{3,2,1,0:T(8,128)}, f32[3,8,4,8,256]{4,3,2,1,0:T(8,128)}) custom-call(f32[8,4,8,256]{3,2,1,0:T(8,128)} %bitcast.12, f32[3,8,4,8,256]{4,3,2,1,0:T(8,128)} %bitcast.10, f32[8,4,8,256]{3,2,1,0:T(8,128)} %bitcast.13, f32[3,8,4,8,256]{4,3,2,1,0:T(8,128)} %bitcast.11, ...), custom_call_target="tpu_custom_call" | custom-call | tf_op jit(solution)/shard_map/step/pallas_call | solution.py:567
  71.1 1.7 %copy.18 = f32[8,32,256]{2,1,0:T(8,128)} copy(f32[8,32,256]{2,1,0:T(8,128)} %bitcast.15) | data formatting | bytes 524288
  72.7 0.0 copy-start.1
  72.7 0.0 copy-start
  72.7 2.2 %copy.19 = f32[3,8,32,256]{3,2,1,0:T(8,128)} copy(f32[3,8,32,256]{3,2,1,0:T(8,128)} %bitcast.9) | data formatting | bytes 1572864
  74.9 0.0 copy-done.1
  74.9 0.7 copy.20
  75.6 0.0 copy-done
  75.6 0.9 %copy.21 = f32[3,8,32,256]{3,2,1,0:T(8,128)} copy(f32[3,8,32,256]{3,2,1,0:T(8,128)S(1)} %bitcast.8) | data formatting | bytes 1572864
Async XLA Ops:
  72.7 2.2 %copy-start.1 = (f32[8,4,8,256]{3,2,1,0:T(8,128)S(1)}, f32[8,4,8,256]{3,2,1,0:T(8,128)}, u32[]{:S(2)}) copy-start(f32[8,4,8,256]{3,2,1,0:T(8,128)} %get-tuple-element.10) | copy-start | bytes 786436
  72.7 2.9 %copy-start = (f32[3,8,4,8,256]{4,3,2,1,0:T(8,128)S(1)}, f32[3,8,4,8,256]{4,3,2,1,0:T(8,128)}, u32[]{:S(2)}) copy-start(f32[3,8,4,8,256]{4,3,2,1,0:T(8,128)} %get-tuple-element.11) | copy-start | bytes 2359300
where the time goes:
time: 76.6 us; the launch traced here: 76.5 us
  Pallas kernels  70.4 us (92%)
  local copies, waits for them, and re-layouts  5.44 us (7%)
    pallas_call x1, Pallas kernels, local(): pl.pallas_call(functools.partial(step_kernel, rows, cols), out_shape=(sca...  70.4 us
    unnamed x8, local copies, waits for them, and re-layouts  5.44 us

commit v1 on v0

v1 whole, which is shorter than its diff:
```python
import functools
import math

import jax
import jax.numpy as jnp
import numpy as np
from jax import lax
from jax.experimental import pallas as pl
from jax.experimental.pallas import tpu as pltpu
from jax.sharding import PartitionSpec as P

gamma_gas = 5.0 / 3.0
time_step = 0.1
coupling = 3.0


def tables(size, chunk):
    index = np.arange(size)
    angle = (index[:, None] * index[None, :] % size) * (2.0 * math.pi / size)
    natural = np.cos(angle) + np.sin(angle)
    order = np.arange(size).reshape(size // chunk, chunk).T.reshape(-1)
    values = 2.0 * np.cos(index * (2.0 * math.pi / size)) - 2.0
    as32 = lambda x: np.ascontiguousarray(x, dtype=np.float32)
    return (as32(natural), as32(natural[:, order]), as32(natural[order, :]), values)


def mm(a, b):
    return lax.dot_general(
        a,
        b,
        (((1,), (0,)), ((), ())),
        precision=lax.Precision.HIGHEST,
        preferred_element_type=jnp.float32,
    )


def exchange_chunks(parts):
    flat = []
    for i in range(4):
        flat.append((parts[i][0], parts[i + 4][0]))
    for i in range(4):
        flat.append((parts[i][1], parts[i + 4][1]))
    rows = parts[0][0].shape[0]
    lane = lax.broadcasted_iota(jnp.int32, (rows, 128), 1)
    for bit, width in ((2, 64), (1, 32)):
        keep = (lane // width) % 2 == 0
        fresh = [None] * 8
        for i in range(8):
            if i & bit:
                continue
            j = i | bit
            low, high = flat[i], flat[j]
            fresh[i] = tuple(
                jnp.where(keep, low[h], pltpu.roll(high[h], width, 1)) for h in range(2)
            )
            fresh[j] = tuple(
                jnp.where(keep, pltpu.roll(low[h], 128 - width, 1), high[h]) for h in range(2)
            )
        flat = fresh
    return flat


def shift_x_down(x):
    return pltpu.roll(x, 1, 1)


def shift_x_up(x):
    return pltpu.roll(x, 255, 1)


def side_terms(side, normal, normal_sq):
    dens, vel_n, vel_a, vel_b, pres, field_a, field_b, inv_dens, sound, hydro = side
    across = field_a * field_a + field_b * field_b
    magnetic = 0.5 * (normal_sq + across)
    energy = hydro + magnetic
    total_p = pres + magnetic
    dot_vb = vel_n * normal + vel_a * field_a + vel_b * field_b
    along = normal_sq * inv_dens
    across = across * inv_dens
    gap = sound - along - across
    fast_sq = sound + along + across + jnp.sqrt(gap * gap + 4.0 * sound * across)
    return (energy, total_p, dot_vb, fast_sq)


def star_state(side, normal, normal_sq, energy, total_p, dot_vb, relative, mass, edge, middle, star_p):
    dens, vel_n, vel_a, vel_b, pres, field_a, field_b = side[:7]
    edge_gap = edge - middle
    inv_gap = 1.0 / edge_gap
    inv_div = 1.0 / (mass * edge_gap - normal_sq)
    star_dens = mass * inv_gap
    offset = normal * (middle - vel_n) * inv_div
    star_va = vel_a - field_a * offset
    star_vb = vel_b - field_b * offset
    factor = (mass * relative - normal_sq) * inv_div
    star_fa = field_a * factor
    star_fb = field_b * factor
    star_dot = middle * normal + star_va * star_fa + star_vb * star_fb
    star_energy = (
        relative * energy - total_p * vel_n + star_p * middle + normal * (dot_vb - star_dot)
    ) * inv_gap
    return (star_dens, star_va, star_vb, star_fa, star_fb, star_dot, star_energy, jnp.sqrt(star_dens))


def hlld_flux(left, right, normal):
    normal_sq = normal * normal
    energy_l, total_l, dot_l, fast_l = side_terms(left, normal, normal_sq)
    energy_r, total_r, dot_r, fast_r = side_terms(right, normal, normal_sq)
    fastest = jnp.sqrt(0.5 * jnp.maximum(fast_l, fast_r))
    slow_edge = jnp.minimum(left[1], right[1]) - fastest
    fast_edge = jnp.maximum(left[1], right[1]) + fastest
    rel_l = slow_edge - left[1]
    rel_r = fast_edge - right[1]
    mass_l = left[0] * rel_l
    mass_r = right[0] * rel_r
    inv_weight = 1.0 / (mass_r - mass_l)
    middle = (mass_r * right[1] - mass_l * left[1] - total_r + total_l) * inv_weight
    star_p = (
        mass_r * total_l - mass_l * total_r + mass_l * mass_r * (right[1] - left[1])
    ) * inv_weight
    star_l = star_state(
        left, normal, normal_sq, energy_l, total_l, dot_l, rel_l, mass_l, slow_edge, middle, star_p
    )
    star_r = star_state(
        right, normal, normal_sq, energy_r, total_r, dot_r, rel_r, mass_r, fast_edge, middle, star_p
    )
    root_l, root_r = star_l[7], star_r[7]
    orient = jnp.where(normal > 0.0, 1.0, jnp.where(normal < 0.0, -1.0, 0.0))
    inv_sum = 1.0 / (root_l + root_r)
    both = root_l * root_r * orient
    dbl_va = (root_l * star_l[1] + root_r * star_r[1] + (star_r[3] - star_l[3]) * orient) * inv_sum
    dbl_vb = (root_l * star_l[2] + root_r * star_r[2] + (star_r[4] - star_l[4]) * orient) * inv_sum
    dbl_fa = (root_l * star_r[3] + root_r * star_l[3] + both * (star_r[1] - star_l[1])) * inv_sum
    dbl_fb = (root_l * star_r[4] + root_r * star_l[4] + both * (star_r[2] - star_l[2])) * inv_sum
    dbl_dot = middle * normal + dbl_va * dbl_fa + dbl_vb * dbl_fb
    on_left = (middle > 0.0) | (slow_edge > 0.0)

    def pick(low, high):
        return jnp.where(on_left, low, high)

    dens, vel_n, vel_a, vel_b = [pick(left[i], right[i]) for i in range(4)]
    field_a, field_b = [pick(left[i], right[i]) for i in (5, 6)]
    energy = pick(energy_l, energy_r)
    total_p = pick(total_l, total_r)
    dot_vb = pick(dot_l, dot_r)
    edge = pick(slow_edge, fast_edge)
    s_dens, s_va, s_vb, s_fa, s_fb, s_dot, s_energy, root = [
        pick(low, high) for low, high in zip(star_l, star_r)
    ]
    way = pick(-1.0, 1.0)
    inner = middle + way * jnp.abs(normal) / root
    ahead = inner > 0.0
    outer = (on_left & (slow_edge > 0.0)) | ~(on_left | (fast_edge > 0.0) | ahead)
    double = (on_left ^ ahead) & ~outer
    d_energy = s_energy + way * root * (s_dot - dbl_dot) * orient
    to_star = jnp.where(outer, 0.0, edge)
    to_double = jnp.where(double, inner, 0.0)
    mass = dens * vel_n
    return (
        mass + to_star * (s_dens - dens),
        mass * vel_n + total_p - normal_sq + to_star * (s_dens * middle - mass),
        mass * vel_a
        - normal * field_a
        + to_star * (s_dens * s_va - dens * vel_a)
        + to_double * (s_dens * (dbl_va - s_va)),
        mass * vel_b
        - normal * field_b
        + to_star * (s_dens * s_vb - dens * vel_b)
        + to_double * (s_dens * (dbl_vb - s_vb)),
        (energy + total_p) * vel_n
        - normal * dot_vb
        + to_star * (s_energy - energy)
        + to_double * (d_energy - s_energy),
        field_a * vel_n - normal * vel_a + to_star * (s_fa - field_a) + to_double * (dbl_fa - s_fa),
        field_b * vel_n - normal * vel_b + to_star * (s_fb - field_b) + to_double * (dbl_fb - s_fb),
    )


def sublane_is(which):
    return lax.broadcasted_iota(jnp.int32, (8, 256), 0) == which


def wrapped(tile, by):
    return (tile + by) % 5 if isinstance(tile, int) else lax.rem(tile + by, 5)


def row_before(load, tile):
    return pltpu.roll(jnp.where(sublane_is(7), load(wrapped(tile, 4)), load(tile)), 1, 0)


def row_after(load, tile):
    return pltpu.roll(jnp.where(sublane_is(0), load(wrapped(tile, 1)), load(tile)), 7, 0)


tangents = ((1, 2), (2, 0), (0, 1))


def cell_pass(state, above, cell, left, plane, tile):
    dens = state[0, plane, tile]
    vel = [state[1 + c, plane, tile] for c in range(3)]
    pres = state[4, plane, tile]
    face = [state[5 + c, plane, tile] for c in range(3)]
    cell[0, plane, tile] = 0.5 * (face[0] + shift_x_up(face[0]))
    field_y = 0.5 * (face[1] + row_after(lambda t: state[6, plane, t], tile))
    field_z = 0.5 * (face[2] + above)
    inv_dens = 1.0 / dens
    sound = gamma_gas * pres * inv_dens
    hydro = pres / (gamma_gas - 1.0) + 0.5 * dens * (
        vel[0] * vel[0] + vel[1] * vel[1] + vel[2] * vel[2]
    )
    for f, value in ((1, field_y), (2, field_z), (3, inv_dens), (4, sound), (5, hydro)):
        cell[f, plane, tile] = value
    members = (dens, *vel, pres, field_y, field_z, inv_dens, sound, hydro)
    for f, value in enumerate(members):
        left[f, plane, tile] = shift_x_down(value)


def flux_pass(direction, state, cell, left_x, flux, plane, tile):
    first, second = tangents[direction]
    members = (
        (state, 0),
        (state, 1 + direction),
        (state, 1 + first),
        (state, 1 + second),
        (state, 4),
        (cell, first),
        (cell, second),
        (cell, 3),
        (cell, 4),
        (cell, 5),
    )
    right = [ref[f, plane, tile] for ref, f in members]
    if direction == 0:
        left = [left_x[f, plane, tile] for f in range(10)]
    elif direction == 1:
        left = [row_before(lambda t, ref=ref, f=f: ref[f, plane, t], tile) for ref, f in members]
    else:
        left = [ref[f, plane - 1, tile] for ref, f in members]
    result = hlld_flux(left, right, state[5 + direction, plane, tile])
    for member in range(7):
        flux[direction, member, plane, tile] = result[member]


def edge_pass(flux, edge, plane, tile):
    flow = flux[1, 6, plane, tile]
    edge[2, plane, tile] = 0.25 * (
        flow
        + shift_x_down(flow)
        - flux[0, 5, plane, tile]
        - row_before(lambda t: flux[0, 5, plane, t], tile)
    )
    edge[0, plane, tile] = 0.25 * (
        flux[2, 6, plane, tile]
        + row_before(lambda t: flux[2, 6, plane, t], tile)
        - flux[1, 5, plane, tile]
        - flux[1, 5, plane - 1, tile]
    )
    flow = flux[2, 5, plane, tile]
    edge[1, plane, tile] = 0.25 * (
        flux[0, 6, plane, tile] + flux[0, 6, plane - 1, tile] - flow - shift_x_down(flow)
    )


def update_pass(state, cell, flux, edge, outs, plane, tile):
    new_dens, new_mom, new_energy, new_face = outs
    own = plane - 1

    def change(slots):
        low = flux[0, slots[0], plane, tile]
        total = shift_x_up(low) - low
        total += row_after(lambda t: flux[1, slots[1], plane, t], tile) - flux[1, slots[1], plane, tile]
        return total + (flux[2, slots[2], plane + 1, tile] - flux[2, slots[2], plane, tile])

    dens = state[0, plane, tile]
    new_dens[own, tile] = dens - time_step * change((0, 0, 0))
    slots = ((1, 3, 2), (2, 1, 3), (3, 2, 1))
    for c in range(3):
        new_mom[c, own, tile] = dens * state[1 + c, plane, tile] - time_step * change(slots[c])
    field = [cell[c, plane, tile] for c in range(3)]
    energy = cell[5, plane, tile] + 0.5 * (
        field[0] * field[0] + field[1] * field[1] + field[2] * field[2]
    )
    new_energy[own, tile] = energy - time_step * change((4, 4, 4))
    low = [edge[c, plane, tile] for c in range(3)]
    above = [edge[c, plane + 1, tile] for c in range(2)]
    new_face[0, own, tile] = state[5, plane, tile] - time_step * (
        row_after(lambda t: edge[2, plane, t], tile) - low[2] - (above[1] - low[1])
    )
    new_face[1, own, tile] = state[6, plane, tile] - time_step * (
        above[0] - low[0] - (shift_x_up(low[2]) - low[2])
    )
    new_face[2, own, tile] = state[7, plane, tile] - time_step * (
        shift_x_up(low[1]) - low[1] - (row_after(lambda t: edge[0, plane, t], tile) - low[0])
    )


def pull_pass(state, phi, outs, plane, tile):
    new_dens, new_mom, new_energy, new_face = outs
    own = plane - 1
    centre = phi[plane, tile]
    load = lambda t: phi[plane, t]
    accel = (
        -0.5 * (shift_x_up(centre) - shift_x_down(centre)),
        -0.5 * (row_after(load, tile) - row_before(load, tile)),
        -0.5 * (phi[plane + 1, tile] - phi[plane - 1, tile]),
    )
    pulled = time_step * state[0, plane, tile]
    work = jnp.zeros_like(centre)
    for c in range(3):
        new_mom[c, own, tile] += pulled * accel[c]
        work += pulled * state[1 + c, plane, tile] * accel[c]
    new_energy[own, tile] += work


def step_kernel(
    rows, cols, dens, vel, pres, face, nat_h, perm_c_h, perm_r_h, eig_z_h, eig_y_h, eig_x_h,
    out_dens, out_mom, out_energy, out_face,
    nat, perm_c, perm_r, eig_z, eig_y, eig_x,
    send_a, recv_a, send_c, recv_c, send_e, recv_e, send_g, recv_g,
    state, cell, left, flux, edge, phi, above_bz, rim_out, rim_in, phi_out, phi_in,
    new_dens, new_mom, new_energy, new_face,
    local_s, over_s, over_r, halo_s, halo_r,
):
    row = lax.axis_index("row")
    col = lax.axis_index("col")
    outs = (new_dens, new_mom, new_energy, new_face)
    barrier = pltpu.get_barrier_semaphore()
    row_up = lax.rem(row + 1, rows)
    row_down = lax.rem(row + rows - 1, rows)
    col_up = lax.rem(col + 1, cols)
    col_down = lax.rem(col + cols - 1, cols)

    def copy(src, dst, send, recv, to_row, to_col):
        return pltpu.make_async_remote_copy(
            src_ref=src, dst_ref=dst, send_sem=send, recv_sem=recv,
            device_id={"row": to_row, "col": to_col}, device_id_type=pl.DeviceIdType.MESH,
        )

    def signal(to_row, to_col):
        pl.semaphore_signal(
            barrier, inc=1, device_id={"row": to_row, "col": to_col},
            device_id_type=pl.DeviceIdType.MESH,
        )

    @pl.loop(1, cols)
    def _(s):
        signal(row, lax.rem(col + s, cols))

    @pl.loop(1, rows)
    def _(s):
        signal(lax.rem(row + s, rows), col)

    reads = [
        pltpu.make_async_copy(src, dst, local_s.at[i])
        for i, (src, dst) in enumerate(
            (
                (dens, state.at[0, 1:9, 0:4]),
                (nat_h, nat),
                (vel, state.at[1:4, 1:9, 0:4]),
                (pres, state.at[4, 1:9, 0:4]),
                (face, state.at[5:8, 1:9, 0:4]),
                (perm_c_h, perm_c),
                (perm_r_h, perm_r),
                (eig_z_h, eig_z),
                (eig_y_h, eig_y),
                (eig_x_h, eig_x),
            )
        )
    ]
    writes = [
        pltpu.make_async_copy(src, dst, local_s.at[i])
        for i, (src, dst) in enumerate(
            (
                (new_dens, out_dens),
                (new_face, out_face),
                (new_mom, out_mom),
                (new_energy, out_energy),
            )
        )
    ]
    for one in reads:
        one.start()

    def row_copy(peer, src, dst, number):
        return copy(src.at[peer], dst.at[row], over_s.at[number], over_r.at[number], peer, col)

    def col_copy(peer, src, dst, number):
        return copy(src.at[:, peer], dst.at[:, col], over_s.at[number], over_r.at[number], row, peer)

    def start_row(*over):
        @pl.loop(1, rows)
        def _(s):
            row_copy(lax.rem(row + s, rows), *over).start()

    def start_col(*over):
        @pl.loop(1, cols)
        def _(s):
            col_copy(lax.rem(col + s, cols), *over).start()

    def all_row(src, dst, number):
        part = slice(0, rows - 1)
        return copy(src.at[part], dst.at[part], over_s.at[number], over_r.at[number], row_up, col)

    def all_col(src, dst, number):
        part = slice(0, cols - 1)
        return copy(src.at[:, part], dst.at[:, part], over_s.at[number], over_r.at[number], row, col_up)

    over_a = (send_a, recv_a, 0)
    over_c = (send_c, recv_c, 1)
    over_e = (send_e, recv_e, 2)
    over_g = (send_g, recv_g, 3)

    def halo(number, src, dst, to_row, to_col):
        return copy(src, dst, halo_s.at[number], halo_r.at[number], to_row, to_col)

    rims = (
        halo(0, rim_out.at[0], rim_in.at[0], row_down, col),
        halo(0, rim_out.at[1], rim_in.at[1], row_up, col),
    )
    rims_all = halo(0, rim_out, rim_in, row_up, col)
    layers = (
        halo(1, state.at[:, 8, 0:4], state.at[:, 0, 0:4], row, col_up),
        halo(2, state.at[:, 1, 0:4], state.at[:, 9, 0:4], row, col_down),
        halo(3, state.at[7, 2, 0:4], above_bz.at[0:4], row, col_down),
    )
    corners = (
        halo(4, state.at[:, 8, 4], state.at[:, 0, 4], row, col_up),
        halo(5, state.at[:, 1, 4], state.at[:, 9, 4], row, col_down),
        halo(6, state.at[7, 2, 4], above_bz.at[4], row, col_down),
    )
    phi_rims = (
        halo(7, phi_out.at[0], phi_in.at[0], row_down, col),
        halo(7, phi_out.at[1], phi_in.at[1], row_up, col),
    )
    phi_rims_all = halo(7, phi_out, phi_in, row_up, col)
    phi_layers = (
        halo(8, phi.at[8, 0:4], phi.at[0, 0:4], row, col_up),
        halo(9, phi.at[1, 0:4], phi.at[9, 0:4], row, col_down),
    )

    def cells(low, high, tiles):
        @pl.loop(low, high)
        def _(plane):
            for tile in tiles:
                cell_pass(state, state[7, plane + 1, tile], cell, left, plane, tile)

    def fluxes(direction, low, high, first, last):
        @pl.loop(low, high)
        def _(plane):
            @pl.loop(first, last)
            def _(tile):
                flux_pass(direction, state, cell, left, flux, plane, tile)

    reads[0].wait()
    reads[1].wait()
    spec = mm(state[0, 1:9, 0:4].reshape(256, 256), nat[...])
    parts = [(spec[32 * z : 32 * z + 32, :128], spec[32 * z : 32 * z + 32, 128:]) for z in range(8)]
    parts = exchange_chunks(parts)
    for r in range(8):
        for h in range(2):
            send_a[r, :, 128 * h : 128 * h + 128] = parts[r][h]
    recv_a[row] = send_a[row]
    for one in reads[2:]:
        one.wait()
    for f in range(8):
        rim_out[0, f] = state[f, 1:9, 0, 0, :]
        rim_out[1, f] = state[f, 1:9, 3, 7, :]
    second = state[6, 1:9, 0, 1, :]
    rim_out[0, 8] = second
    rim_out[1, 8] = second

    cells(1, 8, range(3))
    fluxes(0, 1, 8, 0, 3)
    fluxes(1, 1, 8, 1, 3)
    fluxes(2, 2, 8, 0, 3)
    pl.semaphore_wait(barrier, rows + cols - 2)

    start_row(*over_a)
    for one in rims:
        one.start()
    for one in layers:
        one.start()
    rims_all.wait_recv()
    sub = lax.broadcasted_iota(jnp.int32, (8, 256), 0)
    for f in range(8):
        first = rim_in[0, f]
        last = rim_in[1, f]
        second = rim_in[0, 8]
        for k in range(8):
            tile = jnp.where(sub == 0, first[k : k + 1], last[k : k + 1])
            if f == 6:
                tile = jnp.where(sub == 1, second[k : k + 1], tile)
            state[f, k + 1, 4] = tile
    for one in corners:
        one.start()
    cells(1, 8, range(3, 5))
    fluxes(0, 1, 8, 3, 5)
    fluxes(2, 2, 8, 3, 5)
    all_row(*over_a).wait_recv()

    spec = mm(nat[...], recv_a[...].reshape(256, 256))
    for h in range(2):
        send_c[h] = spec[:, 128 * h : 128 * h + 128].reshape(32, 8, 128)
    recv_c[:, col] = send_c[:, col]
    start_col(*over_c)
    fluxes(1, 1, 8, 3, 5)
    fluxes(1, 1, 8, 0, 1)
    for one in (*layers, *corners):
        one.wait_recv()

    cells(0, 1, range(5))
    cells(8, 9, range(5))
    for tile in range(5):
        cell_pass(state, above_bz[tile], cell, left, 9, tile)
    fluxes(0, 8, 10, 0, 5)
    fluxes(0, 0, 1, 0, 5)
    fluxes(1, 8, 10, 0, 5)
    fluxes(1, 0, 1, 0, 5)
    all_col(*over_c).wait_recv()

    parts = [tuple(recv_c.at[h][:, y, :] for h in range(2)) for y in range(8)]
    parts = exchange_chunks(parts)
    full = jnp.concatenate([jnp.concatenate(list(p), axis=1) for p in parts], axis=0)
    full = mm(perm_c[...], full)
    total = eig_z[...] + (eig_y[pl.ds(col, 1), :] + eig_x[pl.ds(row, 1), :])
    kz = lax.broadcasted_iota(jnp.int32, (256, 256), 0)
    lane = lax.broadcasted_iota(jnp.int32, (256, 256), 1)
    anchor = kz + lane + row + col == 0
    full = full * jnp.where(anchor, 0.0, (coupling / 2.0**24) / jnp.where(anchor, 1.0, total))
    full = mm(perm_r[...], full)
    parts = [(full[32 * z : 32 * z + 32, :128], full[32 * z : 32 * z + 32, 128:]) for z in range(8)]
    parts = exchange_chunks(parts)
    for y in range(8):
        for h in range(2):
            send_e[h, :, y, :] = parts[y][h]
    recv_e[:, col] = send_e[:, col]
    start_col(*over_e)
    fluxes(2, 8, 10, 0, 5)
    fluxes(2, 1, 2, 0, 5)

    @pl.loop(1, 10)
    def _(plane):
        for tile in range(5):
            edge_pass(flux, edge, plane, tile)

    @pl.loop(1, 9)
    def _(plane):
        for tile in range(4):
            update_pass(state, cell, flux, edge, outs, plane, tile)

    for one in writes[:2]:
        one.start()
    all_col(*over_e).wait_recv()
    full = jnp.concatenate([recv_e[h].reshape(256, 128) for h in range(2)], axis=1)
    full = mm(nat[...], full)
    send_g[...] = full.reshape(8, 32, 256)
    recv_g[row] = send_g[row]
    start_row(*over_g)
    all_row(*over_g).wait_recv()
    parts = [(recv_g[r, :, :128], recv_g[r, :, 128:]) for r in range(8)]
    parts = exchange_chunks(parts)
    full = jnp.concatenate([jnp.concatenate(list(p), axis=1) for p in parts], axis=0)
    full = mm(full, nat[...]).reshape(8, 4, 8, 256)
    phi[1:9, 0:4] = full
    phi_out[0] = full[:, 0, 0, :]
    phi_out[1] = full[:, 3, 7, :]
    for one in (*phi_rims, *phi_layers):
        one.start()
    phi_rims_all.wait_recv()
    for k in range(8):
        phi[k + 1, 4] = jnp.where(sub == 0, phi_in[0, k : k + 1], phi_in[1, k : k + 1])

    def pulls(low, high):
        @pl.loop(low, high)
        def _(plane):
            for tile in range(4):
                pull_pass(state, phi, outs, plane, tile)

    pulls(2, 8)
    for one in phi_layers:
        one.wait_recv()
    pulls(1, 2)
    pulls(8, 9)
    for one in writes[2:]:
        one.start()
    all_row(*over_a).wait_send()
    all_row(*over_g).wait_send()
    all_col(*over_c).wait_send()
    all_col(*over_e).wait_send()
    for one in (rims_all, *layers, *corners, phi_rims_all, *phi_layers):
        one.wait_send()
    for one in writes:
        one.wait()


def local(density, velocity, pressure, face_field):
    rows = lax.axis_size("row")
    cols = lax.axis_size("col")
    nat, perm_c, perm_r, values = tables(256, 8)
    eig_z = np.ascontiguousarray(np.broadcast_to(values[:, None], (256, 256)), dtype=np.float32)
    eig_y = np.repeat(values.reshape(32, 8), 32, axis=1).astype(np.float32)
    eig_x = np.tile(values.reshape(8, 32), (1, 8)).astype(np.float32)
    dma = pltpu.SemaphoreType.DMA
    f = jnp.float32
    vm = lambda *shape: pltpu.VMEM(shape, f)
    block = (8, 4, 8, 256)
    scalar = jax.ShapeDtypeStruct(block, f)
    vector = jax.ShapeDtypeStruct((3, *block), f)
    results = pl.pallas_call(
        functools.partial(step_kernel, rows, cols),
        out_shape=(scalar, vector, scalar, vector),
        in_specs=[pl.BlockSpec(memory_space=pl.ANY)] * 10,
        out_specs=(pl.BlockSpec(memory_space=pl.ANY),) * 4,
        scratch_shapes=[
            vm(256, 256), vm(256, 256), vm(256, 256), vm(256, 256), vm(32, 256), vm(8, 256),
            vm(8, 32, 256), vm(8, 32, 256),
            vm(2, 32, 8, 128), vm(2, 32, 8, 128),
            vm(2, 32, 8, 128), vm(2, 32, 8, 128),
            vm(8, 32, 256), vm(8, 32, 256),
            vm(8, 10, 5, 8, 256), vm(6, 10, 5, 8, 256), vm(10, 10, 5, 8, 256),
            vm(3, 7, 10, 5, 8, 256), vm(3, 10, 5, 8, 256),
            vm(10, 5, 8, 256), vm(5, 8, 256),
            vm(2, 9, 8, 256), vm(2, 9, 8, 256),
            vm(2, 8, 256), vm(2, 8, 256),
            vm(*block), vm(3, *block), vm(*block), vm(3, *block),
            dma((10,)), dma((4,)), dma((4,)), dma((10,)), dma((10,)),
        ],
        compiler_params=pltpu.CompilerParams(
            collective_id=0, has_side_effects=True, vmem_limit_bytes=60 * 1024 * 1024
        ),
        name="step",
    )(
        density.reshape(block), velocity.reshape(3, *block), pressure.reshape(block),
        face_field.reshape(3, *block), jnp.asarray(nat), jnp.asarray(perm_c), jnp.asarray(perm_r),
        jnp.asarray(eig_z), jnp.asarray(eig_y), jnp.asarray(eig_x),
    )
    return (
        results[0].reshape(density.shape),
        results[1].reshape(velocity.shape),
        results[2].reshape(density.shape),
        results[3].reshape(velocity.shape),
    )


def solution(mesh):
    in_specs = (
        P("col", "row", None),
        P(None, "col", "row", None),
        P("col", "row", None),
        P(None, "col", "row", None),
    )
    out_specs = (
        P("col", "row", None),
        P(None, "col", "row", None),
        P("col", "row", None),
        P(None, "col", "row", None),
    )
    return jax.shard_map(local, mesh=mesh, in_specs=in_specs, out_specs=out_specs, check_vma=False)
```

time: 76.6 us -> 63.1 us (0.82)
  the two profiles are of different devices: /device:TPU:6 before, /device:TPU:1 now
where the time goes in v1:
time: 63.1 us; the launch traced here: 63 us
  Pallas kernels  56.9 us (90%)
  local copies, waits for them, and re-layouts  5.44 us (9%)
  between operations  0.64 us (1%)
    pallas_call x1, Pallas kernels, local(): pl.pallas_call(functools.partial(step_kernel, rows, cols), out_shape=(sca...  56.9 us
    unnamed x8, local copies, waits for them, and re-layouts  5.44 us

profile of v1, /device:TPU:1, one launch (start us, length us, event | category | flops | bytes accessed | tf_op | source)
XLA Modules:
  0.0 63.0 jit_solution(11523953454074032264)
XLA Ops:
  0.6 56.9 %step.1 = (f32[8,4,8,256]{3,2,1,0:T(8,128)}, f32[3,8,4,8,256]{4,3,2,1,0:T(8,128)}, f32[8,4,8,256]{3,2,1,0:T(8,128)}, f32[3,8,4,8,256]{4,3,2,1,0:T(8,128)}) custom-call(f32[8,4,8,256]{3,2,1,0:T(8,128)} %bitcast.12, f32[3,8,4,8,256]{4,3,2,1,0:T(8,128)} %bitcast.10, f32[8,4,8,256]{3,2,1,0:T(8,128)} %bitcast.13, f32[3,8,4,8,256]{4,3,2,1,0:T(8,128)} %bitcast.11, ...), custom_call_target="tpu_custom_call" | custom-call | tf_op jit(solution)/shard_map/step/pallas_call | solution.py:608
  57.6 1.7 %copy.18 = f32[8,32,256]{2,1,0:T(8,128)} copy(f32[8,32,256]{2,1,0:T(8,128)} %bitcast.15) | data formatting | bytes 524288
  59.2 0.0 copy-start.1
  59.2 0.0 copy-start
  59.2 2.2 %copy.19 = f32[3,8,32,256]{3,2,1,0:T(8,128)} copy(f32[3,8,32,256]{3,2,1,0:T(8,128)} %bitcast.9) | data formatting | bytes 1572864
  61.4 0.0 copy-done.1
  61.4 0.7 %copy.20 = f32[8,32,256]{2,1,0:T(8,128)} copy(f32[8,32,256]{2,1,0:T(8,128)S(1)} %bitcast.14) | data formatting | bytes 524288
  62.1 0.0 copy-done
  62.1 0.9 %copy.21 = f32[3,8,32,256]{3,2,1,0:T(8,128)} copy(f32[3,8,32,256]{3,2,1,0:T(8,128)S(1)} %bitcast.8) | data formatting | bytes 1572864
Async XLA Ops:
  59.2 2.2 %copy-start.1 = (f32[8,4,8,256]{3,2,1,0:T(8,128)S(1)}, f32[8,4,8,256]{3,2,1,0:T(8,128)}, u32[]{:S(2)}) copy-start(f32[8,4,8,256]{3,2,1,0:T(8,128)} %get-tuple-element.10) | copy-start | bytes 786436
  59.2 2.9 %copy-start = (f32[3,8,4,8,256]{4,3,2,1,0:T(8,128)S(1)}, f32[3,8,4,8,256]{4,3,2,1,0:T(8,128)}, u32[]{:S(2)}) copy-start(f32[3,8,4,8,256]{4,3,2,1,0:T(8,128)} %get-tuple-element.11) | copy-start | bytes 2359300

commit v2 on v1

--- a/solution.py
+++ b/solution.py
@@ -34,30 +34,23 @@
     )
 
 
-def exchange_chunks(parts):
-    flat = []
-    for i in range(4):
-        flat.append((parts[i][0], parts[i + 4][0]))
-    for i in range(4):
-        flat.append((parts[i][1], parts[i + 4][1]))
-    rows = parts[0][0].shape[0]
-    lane = lax.broadcasted_iota(jnp.int32, (rows, 128), 1)
+def transpose_chunks(parts):
+    lane = lax.broadcasted_iota(jnp.int32, parts[0].shape, 1)
     for bit, width in ((2, 64), (1, 32)):
         keep = (lane // width) % 2 == 0
-        fresh = [None] * 8
-        for i in range(8):
+        fresh = [None] * 4
+        for i in range(4):
             if i & bit:
                 continue
-            j = i | bit
-            low, high = flat[i], flat[j]
-            fresh[i] = tuple(
-                jnp.where(keep, low[h], pltpu.roll(high[h], width, 1)) for h in range(2)
-            )
-            fresh[j] = tuple(
-                jnp.where(keep, pltpu.roll(low[h], 128 - width, 1), high[h]) for h in range(2)
-            )
-        flat = fresh
-    return flat
+            low, high = parts[i], parts[i | bit]
+            fresh[i] = jnp.where(keep, low, pltpu.roll(high, width, 1))
+            fresh[i | bit] = jnp.where(keep, pltpu.roll(low, 128 - width, 1), high)
+        parts = fresh
+    return parts
+
+
+def side_by_side(low, high):
+    return jnp.concatenate([low, high], axis=1)
 
 
 def shift_x_down(x):
@@ -316,9 +309,9 @@
     out_dens, out_mom, out_energy, out_face,
     nat, perm_c, perm_r, eig_z, eig_y, eig_x,
     send_a, recv_a, send_c, recv_c, send_e, recv_e, send_g, recv_g,
-    state, cell, left, flux, edge, phi, above_bz, rim_out, rim_in, phi_out, phi_in,
+    state, cell, left, flux, edge, phi, above_bz, rim_out, rim_in, cap_out, cap_in,
     new_dens, new_mom, new_energy, new_face,
-    local_s, over_s, over_r, halo_s, halo_r,
+    local_s, over_s, over_r, halo_s, halo_r, ready,
 ):
     row = lax.axis_index("row")
     col = lax.axis_index("col")
@@ -341,13 +334,24 @@
             device_id_type=pl.DeviceIdType.MESH,
         )
 
-    @pl.loop(1, cols)
-    def _(s):
-        signal(row, lax.rem(col + s, cols))
-
     @pl.loop(1, rows)
     def _(s):
         signal(lax.rem(row + s, rows), col)
+
+    @pl.loop(1, 5)
+    def _(s):
+        signal(row, lax.rem(col + s, cols))
+        signal(row, lax.rem(col + cols - s, cols))
+
+    def pass_on(number, by):
+        for step in (by, cols - by):
+            pl.semaphore_signal(
+                ready.at[number], inc=1, device_id={"row": row, "col": lax.rem(col + step, cols)},
+                device_id_type=pl.DeviceIdType.MESH,
+            )
+
+    def passed(number):
+        pl.semaphore_wait(ready.at[number], 2)
 
     reads = [
         pltpu.make_async_copy(src, dst, local_s.at[i])
@@ -380,11 +384,13 @@
     for one in reads:
         one.start()
 
-    def row_copy(peer, src, dst, number):
-        return copy(src.at[peer], dst.at[row], over_s.at[number], over_r.at[number], peer, col)
-
-    def col_copy(peer, src, dst, number):
-        return copy(src.at[:, peer], dst.at[:, col], over_s.at[number], over_r.at[number], row, peer)
+    def row_copy(peer, src, dst, number, h):
+        at = 2 * number + h
+        return copy(src.at[h, peer], dst.at[h, row], over_s.at[at], over_r.at[at], peer, col)
+
+    def col_copy(peer, src, dst, number, h):
+        at = 2 * number + h
+        return copy(src.at[h, peer], dst.at[h, col], over_s.at[at], over_r.at[at], row, peer)
 
     def start_row(*over):
         @pl.loop(1, rows)
@@ -396,13 +402,13 @@
         def _(s):
             col_copy(lax.rem(col + s, cols), *over).start()
 
-    def all_row(src, dst, number):
-        part = slice(0, rows - 1)
-        return copy(src.at[part], dst.at[part], over_s.at[number], over_r.at[number], row_up, col)
-
-    def all_col(src, dst, number):
-        part = slice(0, cols - 1)
-        return copy(src.at[:, part], dst.at[:, part], over_s.at[number], over_r.at[number], row, col_up)
+    def all_row(src, dst, number, h):
+        at, part = 2 * number + h, slice(0, rows - 1)
+        return copy(src.at[h, part], dst.at[h, part], over_s.at[at], over_r.at[at], row_up, col)
+
+    def all_col(src, dst, number, h):
+        at, part = 2 * number + h, slice(0, cols - 1)
+        return copy(src.at[h, part], dst.at[h, part], over_s.at[at], over_r.at[at], row, col_up)
 
     over_a = (send_a, recv_a, 0)
     over_c = (send_c, recv_c, 1)
@@ -427,15 +433,16 @@
         halo(5, state.at[:, 1, 4], state.at[:, 9, 4], row, col_down),
         halo(6, state.at[7, 2, 4], above_bz.at[4], row, col_down),
     )
-    phi_rims = (
-        halo(7, phi_out.at[0], phi_in.at[0], row_down, col),
-        halo(7, phi_out.at[1], phi_in.at[1], row_up, col),
-    )
-    phi_rims_all = halo(7, phi_out, phi_in, row_up, col)
-    phi_layers = (
-        halo(8, phi.at[8, 0:4], phi.at[0, 0:4], row, col_up),
-        halo(9, phi.at[1, 0:4], phi.at[9, 0:4], row, col_down),
-    )
+    caps = []
+    for number, (plane, to_col) in enumerate(((0, col_down), (1, col_up))):
+        caps.append(
+            (
+                lambda peer, n=number, c=to_col: copy(
+                    cap_out.at[n, peer], cap_in.at[n, row], halo_s.at[7 + n], halo_r.at[7 + n], peer, c
+                ),
+                halo(7 + number, cap_out.at[number], cap_in.at[number], row, to_col),
+            )
+        )
 
     def cells(low, high, tiles):
         @pl.loop(low, high)
@@ -453,12 +460,14 @@
     reads[0].wait()
     reads[1].wait()
     spec = mm(state[0, 1:9, 0:4].reshape(256, 256), nat[...])
-    parts = [(spec[32 * z : 32 * z + 32, :128], spec[32 * z : 32 * z + 32, 128:]) for z in range(8)]
-    parts = exchange_chunks(parts)
-    for r in range(8):
-        for h in range(2):
-            send_a[r, :, 128 * h : 128 * h + 128] = parts[r][h]
-    recv_a[row] = send_a[row]
+    for h in range(2):
+        for g in range(2):
+            parts = [
+                spec[32 * z : 32 * z + 32, 128 * g : 128 * g + 128] for z in range(4 * h, 4 * h + 4)
+            ]
+            for r, part in enumerate(transpose_chunks(parts)):
+                send_a[h, 4 * g + r] = part
+        recv_a[h, row] = send_a[h, row]
     for one in reads[2:]:
         one.wait()
     for f in range(8):
@@ -469,16 +478,17 @@
     rim_out[1, 8] = second
 
     cells(1, 8, range(3))
-    fluxes(0, 1, 8, 0, 3)
-    fluxes(1, 1, 8, 1, 3)
-    fluxes(2, 2, 8, 0, 3)
-    pl.semaphore_wait(barrier, rows + cols - 2)
-
-    start_row(*over_a)
+    fluxes(0, 1, 4, 0, 3)
+    pl.semaphore_wait(barrier, rows - 1 + 8)
+
+    for h in range(2):
+        start_row(*over_a, h)
     for one in rims:
         one.start()
     for one in layers:
         one.start()
+    pass_on(0, 4)
+    fluxes(0, 4, 8, 0, 3)
     rims_all.wait_recv()
     sub = lax.broadcasted_iota(jnp.int32, (8, 256), 0)
     for f in range(8):
@@ -492,21 +502,47 @@
             state[f, k + 1, 4] = tile
     for one in corners:
         one.start()
+    passed(0)
+    pass_on(1, 8)
+    fluxes(1, 1, 8, 1, 3)
+    fluxes(2, 2, 8, 0, 3)
+
+    passed(1)
+    for h in range(2):
+        all_row(*over_a, h).wait_recv()
+        spec = mm(nat[...], recv_a[h].reshape(256, 128))
+        send_c[h] = spec.reshape(32, 8, 128)
+        recv_c[h, col] = send_c[h, col]
+        start_col(*over_c, h)
     cells(1, 8, range(3, 5))
     fluxes(0, 1, 8, 3, 5)
     fluxes(2, 2, 8, 3, 5)
-    all_row(*over_a).wait_recv()
-
-    spec = mm(nat[...], recv_a[...].reshape(256, 256))
-    for h in range(2):
-        send_c[h] = spec[:, 128 * h : 128 * h + 128].reshape(32, 8, 128)
-    recv_c[:, col] = send_c[:, col]
-    start_col(*over_c)
     fluxes(1, 1, 8, 3, 5)
     fluxes(1, 1, 8, 0, 1)
+
+    for h in range(2):
+        all_col(*over_c, h).wait_recv()
+    stacked = []
+    for h in range(2):
+        low = transpose_chunks([recv_c.at[h][:, y, :] for y in range(4)])
+        high = transpose_chunks([recv_c.at[h][:, y, :] for y in range(4, 8)])
+        stacked += [side_by_side(*pair) for pair in zip(low, high)]
+    full = mm(perm_c[...], jnp.concatenate(stacked, axis=0))
+    total = eig_z[...] + (eig_y[pl.ds(col, 1), :] + eig_x[pl.ds(row, 1), :])
+    kz = lax.broadcasted_iota(jnp.int32, (256, 256), 0)
+    lane = lax.broadcasted_iota(jnp.int32, (256, 256), 1)
+    anchor = kz + lane + row + col == 0
+    full = full * jnp.where(anchor, 0.0, (coupling / 2.0**24) / jnp.where(anchor, 1.0, total))
+    for h in range(2):
+        back = mm(perm_r[128 * h : 128 * h + 128], full)
+        for g in range(2):
+            parts = [back[32 * z : 32 * z + 32, 128 * g : 128 * g + 128] for z in range(4)]
+            for y, part in enumerate(transpose_chunks(parts)):
+                send_e[h, :, 4 * g + y, :] = part
+        recv_e[h, col] = send_e[h, col]
+        start_col(*over_e, h)
     for one in (*layers, *corners):
         one.wait_recv()
-
     cells(0, 1, range(5))
     cells(8, 9, range(5))
     for tile in range(5):
@@ -515,25 +551,6 @@
     fluxes(0, 0, 1, 0, 5)
     fluxes(1, 8, 10, 0, 5)
     fluxes(1, 0, 1, 0, 5)
-    all_col(*over_c).wait_recv()
-
-    parts = [tuple(recv_c.at[h][:, y, :] for h in range(2)) for y in range(8)]
-    parts = exchange_chunks(parts)
-    full = jnp.concatenate([jnp.concatenate(list(p), axis=1) for p in parts], axis=0)
-    full = mm(perm_c[...], full)
-    total = eig_z[...] + (eig_y[pl.ds(col, 1), :] + eig_x[pl.ds(row, 1), :])
-    kz = lax.broadcasted_iota(jnp.int32, (256, 256), 0)
-    lane = lax.broadcasted_iota(jnp.int32, (256, 256), 1)
-    anchor = kz + lane + row + col == 0
-    full = full * jnp.where(anchor, 0.0, (coupling / 2.0**24) / jnp.where(anchor, 1.0, total))
-    full = mm(perm_r[...], full)
-    parts = [(full[32 * z : 32 * z + 32, :128], full[32 * z : 32 * z + 32, 128:]) for z in range(8)]
-    parts = exchange_chunks(parts)
-    for y in range(8):
-        for h in range(2):
-            send_e[h, :, y, :] = parts[y][h]
-    recv_e[:, col] = send_e[:, col]
-    start_col(*over_e)
     fluxes(2, 8, 10, 0, 5)
     fluxes(2, 1, 2, 0, 5)
 
@@ -549,25 +566,40 @@
 
     for one in writes[:2]:
         one.start()
-    all_col(*over_e).wait_recv()
-    full = jnp.concatenate([recv_e[h].reshape(256, 128) for h in range(2)], axis=1)
-    full = mm(nat[...], full)
-    send_g[...] = full.reshape(8, 32, 256)
-    recv_g[row] = send_g[row]
-    start_row(*over_g)
-    all_row(*over_g).wait_recv()
-    parts = [(recv_g[r, :, :128], recv_g[r, :, 128:]) for r in range(8)]
-    parts = exchange_chunks(parts)
-    full = jnp.concatenate([jnp.concatenate(list(p), axis=1) for p in parts], axis=0)
-    full = mm(full, nat[...]).reshape(8, 4, 8, 256)
-    phi[1:9, 0:4] = full
-    phi_out[0] = full[:, 0, 0, :]
-    phi_out[1] = full[:, 3, 7, :]
-    for one in (*phi_rims, *phi_layers):
-        one.start()
-    phi_rims_all.wait_recv()
-    for k in range(8):
-        phi[k + 1, 4] = jnp.where(sub == 0, phi_in[0, k : k + 1], phi_in[1, k : k + 1])
+
+    low_tile = lax.broadcasted_iota(jnp.int32, (8, 128), 0) == 7
+    chunk = lax.broadcasted_iota(jnp.int32, (8, 128), 1) // 32
+    for h in range(2):
+        all_col(*over_e, h).wait_recv()
+        back = mm(nat[...], recv_e[h].reshape(256, 128))
+        tiles = [back[8 * t : 8 * t + 8] for t in range(32)]
+        for r in range(8):
+            send_g[h, r, :32] = back[32 * r : 32 * r + 32]
+            send_g[h, r, 32:] = jnp.where(low_tile, tiles[(4 * r + 31) % 32], tiles[(4 * r + 4) % 32])
+        recv_g[h, row] = send_g[h, row]
+        start_row(*over_g, h)
+        for r in range(8):
+            packed = tiles[4 * r + 3 * h]
+            for t in range(4):
+                if t != 3 * h:
+                    shift = 32 * (t - 3 * h) % 128
+                    packed = jnp.where(chunk == t, pltpu.roll(tiles[4 * r + t], shift, 1), packed)
+            cap_out[h, r] = packed
+
+        @pl.loop(0, rows)
+        def _(s, one=caps[h][0]):
+            one(lax.rem(row + s, rows)).start()
+
+    def planes_of(parts, rows_each):
+        low = transpose_chunks(parts[:4])
+        high = transpose_chunks(parts[4:])
+        full = jnp.concatenate([side_by_side(*pair) for pair in zip(low, high)], axis=0)
+        return mm(full, nat[...])
+
+    for h in range(2):
+        all_row(*over_g, h).wait_recv()
+        full = planes_of([recv_g[h, r] for r in range(8)], 40)
+        phi[1 + 4 * h : 5 + 4 * h] = full.reshape(4, 5, 8, 256)
 
     def pulls(low, high):
         @pl.loop(low, high)
@@ -576,20 +608,44 @@
                 pull_pass(state, phi, outs, plane, tile)
 
     pulls(2, 8)
-    for one in phi_layers:
-        one.wait_recv()
+    for number, plane in ((0, 9), (1, 0)):
+        caps[number][1].wait_recv()
+        full = planes_of([cap_in[number, r] for r in range(8)], 8)
+        phi[plane, 0:4] = full.reshape(4, 8, 256)
     pulls(1, 2)
     pulls(8, 9)
     for one in writes[2:]:
         one.start()
-    all_row(*over_a).wait_send()
-    all_row(*over_g).wait_send()
-    all_col(*over_c).wait_send()
-    all_col(*over_e).wait_send()
-    for one in (rims_all, *layers, *corners, phi_rims_all, *phi_layers):
+    for h in range(2):
+        all_row(*over_a, h).wait_send()
+        all_row(*over_g, h).wait_send()
+        all_col(*over_c, h).wait_send()
+        all_col(*over_e, h).wait_send()
+    for one in (rims_all, *layers, *corners, caps[0][1], caps[1][1]):
         one.wait_send()
     for one in writes:
         one.wait()
+
+
+def write_kernel(*refs):
+    sources, targets, sems = refs[:4], refs[4:8], refs[8]
+    moves = [pltpu.make_async_copy(s, t, sems.at[i]) for i, (s, t) in enumerate(zip(sources, targets))]
+    for one in moves:
+        one.start()
+    for one in moves:
+        one.wait()
+
+
+def written(*results):
+    return pl.pallas_call(
+        write_kernel,
+        out_shape=tuple(jax.ShapeDtypeStruct(r.shape, r.dtype) for r in results),
+        in_specs=[pl.BlockSpec(memory_space=pl.ANY)] * 4,
+        out_specs=(pl.BlockSpec(memory_space=pltpu.HBM),) * 4,
+        scratch_shapes=[pltpu.SemaphoreType.DMA((4,))],
+        compiler_params=pltpu.CompilerParams(vmem_limit_bytes=1024 * 1024),
+        name="write",
+    )(*results)
 
 
 def local(density, velocity, pressure, face_field):
@@ -608,31 +664,38 @@
     results = pl.pallas_call(
         functools.partial(step_kernel, rows, cols),
         out_shape=(scalar, vector, scalar, vector),
-        in_specs=[pl.BlockSpec(memory_space=pl.ANY)] * 10,
+        in_specs=[pl.BlockSpec(memory_space=pltpu.HBM)] * 10,
         out_specs=(pl.BlockSpec(memory_space=pl.ANY),) * 4,
         scratch_shapes=[
             vm(256, 256), vm(256, 256), vm(256, 256), vm(256, 256), vm(32, 256), vm(8, 256),
-            vm(8, 32, 256), vm(8, 32, 256),
+            vm(2, 8, 32, 128), vm(2, 8, 32, 128),
             vm(2, 32, 8, 128), vm(2, 32, 8, 128),
             vm(2, 32, 8, 128), vm(2, 32, 8, 128),
-            vm(8, 32, 256), vm(8, 32, 256),
+            vm(2, 8, 40, 128), vm(2, 8, 40, 128),
             vm(8, 10, 5, 8, 256), vm(6, 10, 5, 8, 256), vm(10, 10, 5, 8, 256),
             vm(3, 7, 10, 5, 8, 256), vm(3, 10, 5, 8, 256),
             vm(10, 5, 8, 256), vm(5, 8, 256),
             vm(2, 9, 8, 256), vm(2, 9, 8, 256),
-            vm(2, 8, 256), vm(2, 8, 256),
+            vm(2, 8, 8, 128), vm(2, 8, 8, 128),
             vm(*block), vm(3, *block), vm(*block), vm(3, *block),
-            dma((10,)), dma((4,)), dma((4,)), dma((10,)), dma((10,)),
+            dma((10,)), dma((8,)), dma((8,)), dma((9,)), dma((9,)),
+            pltpu.SemaphoreType.REGULAR((2,)),
         ],
         compiler_params=pltpu.CompilerParams(
-            collective_id=0, has_side_effects=True, vmem_limit_bytes=60 * 1024 * 1024
+            collective_id=0, has_side_effects=True, vmem_limit_bytes=40 * 1024 * 1024
         ),
         name="step",
     )(
-        density.reshape(block), velocity.reshape(3, *block), pressure.reshape(block),
-        face_field.reshape(3, *block), jnp.asarray(nat), jnp.asarray(perm_c), jnp.asarray(perm_r),
-        jnp.asarray(eig_z), jnp.asarray(eig_y), jnp.asarray(eig_x),
-    )
+        *(
+            pltpu.with_memory_space_constraint(x, pltpu.HBM)
+            for x in (
+                density.reshape(block), velocity.reshape(3, *block), pressure.reshape(block),
+                face_field.reshape(3, *block), jnp.asarray(nat), jnp.asarray(perm_c),
+                jnp.asarray(perm_r), jnp.asarray(eig_z), jnp.asarray(eig_y), jnp.asarray(eig_x),
+            )
+        )
+    )
+    results = written(*results)
     return (
         results[0].reshape(density.shape),
         results[1].reshape(velocity.shape),

time: 63.1 us -> 52.6 us (0.83)
  local copies, waits for them, and re-layouts: 5.44 us -> 0 us
  Pallas kernels: 56.9 us -> 51.9 us
    pallas_call x1, Pallas kernels: 56.9 us -> 50.5 us  [local(): pl.pallas_call(functools.partial(step_kernel, rows, cols), out_shape=(sca...]
    unnamed x8 -> x0, local copies, waits for them, and re-layouts: 5.44 us -> none
    pallas_call x0 -> x1, Pallas kernels: none -> 1.35 us  [written(): pl.pallas_call(write_kernel, out_shape=tuple((jax.ShapeDtypeStruct(r.shap...]
where the time goes in v2:
time: 52.6 us; the launch traced here: 52.5 us
  Pallas kernels  51.9 us (99%)
  between operations  0.64 us (1%)
    pallas_call x1, Pallas kernels, local(): pl.pallas_call(functools.partial(step_kernel, rows, cols), out_shape=(sca...  50.5 us
    pallas_call x1, Pallas kernels, written(): pl.pallas_call(write_kernel, out_shape=tuple((jax.ShapeDtypeStruct(r.shap...  1.35 us

profile of v2, /device:TPU:1, one launch (start us, length us, event | category | flops | bytes accessed | tf_op | source)
XLA Modules:
  0.0 52.5 jit_solution(13011985387877285895)
XLA Ops:
  0.6 50.5 %step.1 = (f32[8,4,8,256]{3,2,1,0:T(8,128)S(1)}, f32[3,8,4,8,256]{4,3,2,1,0:T(8,128)S(1)}, f32[8,4,8,256]{3,2,1,0:T(8,128)S(1)}, f32[3,8,4,8,256]{4,3,2,1,0:T(8,128)S(1)}) custom-call(f32[8,4,8,256]{3,2,1,0:T(8,128)} %bitcast.10, f32[3,8,4,8,256]{4,3,2,1,0:T(8,128)} %bitcast.8, f32[8,4,8,256]{3,2,1,0:T(8,128)} %bitcast.11, f32[3,8,4,8,256]{4,3,2,1,0:T(8,128)} %bitcast.9, ...), custom_call_target="tpu_custom_call" | custom-call | tf_op jit(solution)/shard_map/step/pallas_call | solution.py:664
  51.2 1.3 %write.1 = (f32[8,4,8,256]{3,2,1,0:T(8,128)}, f32[3,8,4,8,256]{4,3,2,1,0:T(8,128)}, f32[8,4,8,256]{3,2,1,0:T(8,128)}, f32[3,8,4,8,256]{4,3,2,1,0:T(8,128)}) custom-call(f32[8,4,8,256]{3,2,1,0:T(8,128)S(1)} %get-tuple-element.12.refs_0_, f32[3,8,4,8,256]{4,3,2,1,0:T(8,128)S(1)} %get-tuple-element.13.refs_1_, f32[8,4,8,256]{3,2,1,0:T(8,128)S(1)} %get-tuple-element.14.refs_2_, ...), custom_call_target="tpu_custom_call" | custom-call | tf_op jit(solution)/shard_map/write/pallas_call | solution.py:640

commit v3 on v2

--- a/solution.py
+++ b/solution.py
@@ -398,9 +398,15 @@
             row_copy(lax.rem(row + s, rows), *over).start()
 
     def start_col(*over):
-        @pl.loop(1, cols)
-        def _(s):
-            col_copy(lax.rem(col + s, cols), *over).start()
+        half, quarter = cols // 2, cols // 4
+
+        @pl.loop(0, half - 1)
+        def _(i):
+            far = quarter + (i + 1) // 2 * (1 - 2 * lax.rem(i, 2))
+            col_copy(lax.rem(col + far, cols), *over).start()
+            col_copy(lax.rem(col + half + far, cols), *over).start()
+
+        col_copy(lax.rem(col + half, cols), *over).start()
 
     def all_row(src, dst, number, h):
         at, part = 2 * number + h, slice(0, rows - 1)
@@ -468,6 +474,11 @@
             for r, part in enumerate(transpose_chunks(parts)):
                 send_a[h, 4 * g + r] = part
         recv_a[h, row] = send_a[h, row]
+    pl.semaphore_wait(barrier, rows - 1 + 8)
+
+    for h in range(2):
+        start_row(*over_a, h)
+    pass_on(0, 4)
     for one in reads[2:]:
         one.wait()
     for f in range(8):
@@ -477,18 +488,15 @@
     rim_out[0, 8] = second
     rim_out[1, 8] = second
 
-    cells(1, 8, range(3))
-    fluxes(0, 1, 4, 0, 3)
-    pl.semaphore_wait(barrier, rows - 1 + 8)
-
-    for h in range(2):
-        start_row(*over_a, h)
     for one in rims:
         one.start()
+
+    cells(1, 8, range(3))
+    passed(0)
+    pass_on(1, 8)
     for one in layers:
         one.start()
-    pass_on(0, 4)
-    fluxes(0, 4, 8, 0, 3)
+    fluxes(0, 1, 5, 0, 3)
     rims_all.wait_recv()
     sub = lax.broadcasted_iota(jnp.int32, (8, 256), 0)
     for f in range(8):
@@ -502,10 +510,13 @@
             state[f, k + 1, 4] = tile
     for one in corners:
         one.start()
-    passed(0)
-    pass_on(1, 8)
-    fluxes(1, 1, 8, 1, 3)
-    fluxes(2, 2, 8, 0, 3)
+    total = eig_z[...] + (eig_y[pl.ds(col, 1), :] + eig_x[pl.ds(row, 1), :])
+    kz = lax.broadcasted_iota(jnp.int32, (256, 256), 0)
+    lane = lax.broadcasted_iota(jnp.int32, (256, 256), 1)
+    anchor = kz + lane + row + col == 0
+    eig_z[...] = jnp.where(anchor, 0.0, (coupling / 2.0**24) / jnp.where(anchor, 1.0, total))
+
+    fluxes(0, 5, 8, 0, 3)
 
     passed(1)
     for h in range(2):
@@ -514,11 +525,11 @@
         send_c[h] = spec.reshape(32, 8, 128)
         recv_c[h, col] = send_c[h, col]
         start_col(*over_c, h)
+    fluxes(1, 1, 8, 1, 3)
+    fluxes(2, 2, 8, 0, 3)
     cells(1, 8, range(3, 5))
     fluxes(0, 1, 8, 3, 5)
     fluxes(2, 2, 8, 3, 5)
-    fluxes(1, 1, 8, 3, 5)
-    fluxes(1, 1, 8, 0, 1)
 
     for h in range(2):
         all_col(*over_c, h).wait_recv()
@@ -528,11 +539,7 @@
         high = transpose_chunks([recv_c.at[h][:, y, :] for y in range(4, 8)])
         stacked += [side_by_side(*pair) for pair in zip(low, high)]
     full = mm(perm_c[...], jnp.concatenate(stacked, axis=0))
-    total = eig_z[...] + (eig_y[pl.ds(col, 1), :] + eig_x[pl.ds(row, 1), :])
-    kz = lax.broadcasted_iota(jnp.int32, (256, 256), 0)
-    lane = lax.broadcasted_iota(jnp.int32, (256, 256), 1)
-    anchor = kz + lane + row + col == 0
-    full = full * jnp.where(anchor, 0.0, (coupling / 2.0**24) / jnp.where(anchor, 1.0, total))
+    full = full * eig_z[...]
     for h in range(2):
         back = mm(perm_r[128 * h : 128 * h + 128], full)
         for g in range(2):
@@ -541,6 +548,8 @@
                 send_e[h, :, 4 * g + y, :] = part
         recv_e[h, col] = send_e[h, col]
         start_col(*over_e, h)
+    fluxes(1, 1, 8, 3, 5)
+    fluxes(1, 1, 8, 0, 1)
     for one in (*layers, *corners):
         one.wait_recv()
     cells(0, 1, range(5))
@@ -551,21 +560,6 @@
     fluxes(0, 0, 1, 0, 5)
     fluxes(1, 8, 10, 0, 5)
     fluxes(1, 0, 1, 0, 5)
-    fluxes(2, 8, 10, 0, 5)
-    fluxes(2, 1, 2, 0, 5)
-
-    @pl.loop(1, 10)
-    def _(plane):
-        for tile in range(5):
-            edge_pass(flux, edge, plane, tile)
-
-    @pl.loop(1, 9)
-    def _(plane):
-        for tile in range(4):
-            update_pass(state, cell, flux, edge, outs, plane, tile)
-
-    for one in writes[:2]:
-        one.start()
 
     low_tile = lax.broadcasted_iota(jnp.int32, (8, 128), 0) == 7
     chunk = lax.broadcasted_iota(jnp.int32, (8, 128), 1) // 32
@@ -590,24 +584,42 @@
         def _(s, one=caps[h][0]):
             one(lax.rem(row + s, rows)).start()
 
+    def pulls(low, high):
+        @pl.loop(low, high)
+        def _(plane):
+            for tile in range(4):
+                pull_pass(state, phi, outs, plane, tile)
+
     def planes_of(parts, rows_each):
         low = transpose_chunks(parts[:4])
         high = transpose_chunks(parts[4:])
         full = jnp.concatenate([side_by_side(*pair) for pair in zip(low, high)], axis=0)
         return mm(full, nat[...])
 
+    fluxes(2, 8, 10, 0, 5)
+    fluxes(2, 1, 2, 0, 5)
+
+    @pl.loop(1, 10)
+    def _(plane):
+        for tile in range(5):
+            edge_pass(flux, edge, plane, tile)
+
+    @pl.loop(1, 9)
+    def _(plane):
+        for tile in range(4):
+            update_pass(state, cell, flux, edge, outs, plane, tile)
+
+    for one in writes[:2]:
+        one.start()
+
     for h in range(2):
         all_row(*over_g, h).wait_recv()
         full = planes_of([recv_g[h, r] for r in range(8)], 40)
         phi[1 + 4 * h : 5 + 4 * h] = full.reshape(4, 5, 8, 256)
-
-    def pulls(low, high):
-        @pl.loop(low, high)
-        def _(plane):
-            for tile in range(4):
-                pull_pass(state, phi, outs, plane, tile)
-
-    pulls(2, 8)
+        if h == 0:
+            pulls(2, 4)
+
+    pulls(4, 8)
     for number, plane in ((0, 9), (1, 0)):
         caps[number][1].wait_recv()
         full = planes_of([cap_in[number, r] for r in range(8)], 8)

time: 52.6 us -> 49.8 us (0.947)
  Pallas kernels: 51.9 us -> 49.1 us
    pallas_call x1, Pallas kernels: 50.5 us -> 47.8 us  [local(): pl.pallas_call(functools.partial(step_kernel, rows, cols), out_shape=(sca...]
where the time goes in v3:
time: 49.8 us; the launch traced here: 49.7 us
  Pallas kernels  49.1 us (99%)
  between operations  0.64 us (1%)
    pallas_call x1, Pallas kernels, local(): pl.pallas_call(functools.partial(step_kernel, rows, cols), out_shape=(sca...  47.8 us
    pallas_call x1, Pallas kernels, written(): pl.pallas_call(write_kernel, out_shape=tuple((jax.ShapeDtypeStruct(r.shap...  1.35 us

profile of v3, /device:TPU:1, one launch (start us, length us, event | category | flops | bytes accessed | tf_op | source)
XLA Modules:
  0.0 49.7 jit_solution(15720591307145077681)
XLA Ops:
  0.6 47.8 %step.1 = (f32[8,4,8,256]{3,2,1,0:T(8,128)S(1)}, f32[3,8,4,8,256]{4,3,2,1,0:T(8,128)S(1)}, f32[8,4,8,256]{3,2,1,0:T(8,128)S(1)}, f32[3,8,4,8,256]{4,3,2,1,0:T(8,128)S(1)}) custom-call(f32[8,4,8,256]{3,2,1,0:T(8,128)} %bitcast.10, f32[3,8,4,8,256]{4,3,2,1,0:T(8,128)} %bitcast.8, f32[8,4,8,256]{3,2,1,0:T(8,128)} %bitcast.11, f32[3,8,4,8,256]{4,3,2,1,0:T(8,128)} %bitcast.9, ...), custom_call_target="tpu_custom_call" | custom-call | tf_op jit(solution)/shard_map/step/pallas_call | solution.py:676
  48.4 1.3 %write.1 = (f32[8,4,8,256]{3,2,1,0:T(8,128)}, f32[3,8,4,8,256]{4,3,2,1,0:T(8,128)}, f32[8,4,8,256]{3,2,1,0:T(8,128)}, f32[3,8,4,8,256]{4,3,2,1,0:T(8,128)}) custom-call(f32[8,4,8,256]{3,2,1,0:T(8,128)S(1)} %get-tuple-element.12.refs_0_, f32[3,8,4,8,256]{4,3,2,1,0:T(8,128)S(1)} %get-tuple-element.13.refs_1_, f32[8,4,8,256]{3,2,1,0:T(8,128)S(1)} %get-tuple-element.14.refs_2_, ...), custom_call_target="tpu_custom_call" | custom-call | tf_op jit(solution)/shard_map/write/pallas_call | solution.py:652

commit v4 on v3

--- a/solution.py
+++ b/solution.py
@@ -381,7 +381,7 @@
             )
         )
     ]
-    for one in reads:
+    for one in reads[:2]:
         one.start()
 
     def row_copy(peer, src, dst, number, h):
@@ -463,8 +463,10 @@
             def _(tile):
                 flux_pass(direction, state, cell, left, flux, plane, tile)
 
-    reads[0].wait()
-    reads[1].wait()
+    for one in reads[:2]:
+        one.wait()
+    for one in reads[2:]:
+        one.start()
     spec = mm(state[0, 1:9, 0:4].reshape(256, 256), nat[...])
     for h in range(2):
         for g in range(2):
@@ -560,6 +562,14 @@
     fluxes(0, 0, 1, 0, 5)
     fluxes(1, 8, 10, 0, 5)
     fluxes(1, 0, 1, 0, 5)
+    fluxes(2, 8, 10, 0, 5)
+    fluxes(2, 1, 2, 0, 5)
+
+    @pl.loop(1, 10)
+    def _(plane):
+        for tile in range(5):
+            edge_pass(flux, edge, plane, tile)
+
 
     low_tile = lax.broadcasted_iota(jnp.int32, (8, 128), 0) == 7
     chunk = lax.broadcasted_iota(jnp.int32, (8, 128), 1) // 32
@@ -595,14 +605,6 @@
         high = transpose_chunks(parts[4:])
         full = jnp.concatenate([side_by_side(*pair) for pair in zip(low, high)], axis=0)
         return mm(full, nat[...])
-
-    fluxes(2, 8, 10, 0, 5)
-    fluxes(2, 1, 2, 0, 5)
-
-    @pl.loop(1, 10)
-    def _(plane):
-        for tile in range(5):
-            edge_pass(flux, edge, plane, tile)
 
     @pl.loop(1, 9)
     def _(plane):

time: 49.8 us -> 49.6 us (level)
  Pallas kernels: 49.1 us -> 48.5 us
    pallas_call x1, Pallas kernels: 47.8 us -> 47.2 us  [local(): pl.pallas_call(functools.partial(step_kernel, rows, cols), out_shape=(sca...]
where the time goes in v4:
time: 49.6 us; the launch traced here: 49.2 us
  Pallas kernels  48.5 us (98%)
  between operations  0.64 us (1%)
    pallas_call x1, Pallas kernels, local(): pl.pallas_call(functools.partial(step_kernel, rows, cols), out_shape=(sca...  47.2 us
    pallas_call x1, Pallas kernels, written(): pl.pallas_call(write_kernel, out_shape=tuple((jax.ShapeDtypeStruct(r.shap...  1.35 us

profile of v4, /device:TPU:1, one launch (start us, length us, event | category | flops | bytes accessed | tf_op | source)
XLA Modules:
  0.0 49.2 jit_solution(11549109347602832376)
XLA Ops:
  0.6 47.2 %step.1 = (f32[8,4,8,256]{3,2,1,0:T(8,128)S(1)}, f32[3,8,4,8,256]{4,3,2,1,0:T(8,128)S(1)}, f32[8,4,8,256]{3,2,1,0:T(8,128)S(1)}, f32[3,8,4,8,256]{4,3,2,1,0:T(8,128)S(1)}) custom-call(f32[8,4,8,256]{3,2,1,0:T(8,128)} %bitcast.10, f32[3,8,4,8,256]{4,3,2,1,0:T(8,128)} %bitcast.8, f32[8,4,8,256]{3,2,1,0:T(8,128)} %bitcast.11, f32[3,8,4,8,256]{4,3,2,1,0:T(8,128)} %bitcast.9, ...), custom_call_target="tpu_custom_call" | custom-call | tf_op jit(solution)/shard_map/step/pallas_call | solution.py:678
  47.8 1.3 %write.1 = (f32[8,4,8,256]{3,2,1,0:T(8,128)}, f32[3,8,4,8,256]{4,3,2,1,0:T(8,128)}, f32[8,4,8,256]{3,2,1,0:T(8,128)}, f32[3,8,4,8,256]{4,3,2,1,0:T(8,128)}) custom-call(f32[8,4,8,256]{3,2,1,0:T(8,128)S(1)} %get-tuple-element.12.refs_0_, f32[3,8,4,8,256]{4,3,2,1,0:T(8,128)S(1)} %get-tuple-element.13.refs_1_, f32[8,4,8,256]{3,2,1,0:T(8,128)S(1)} %get-tuple-element.14.refs_2_, ...), custom_call_target="tpu_custom_call" | custom-call | tf_op jit(solution)/shard_map/write/pallas_call | solution.py:654
